TPU v7x, 32 devices: a whole 2x2x4 slice. The times are simulated.
32 devices in a mesh: grp: 4 (over y, core), dom: 8 (over z, x).
Axes of the slice: x: 2, y: 2, z: 4, core: 2. Of those that a mesh axis runs over, the one named last changes fastest.
Arguments:
- element_state: float32 [56, 9, 20480], P(None, None, ('grp', 'dom')), may hold values from -6 to 6
- stiffness: float32 [3, 56, 56], replicated, may hold values from -0.75 to 0.75
- flux_local: float32 [4, 56, 56], replicated, may hold values from -0.75 to 0.75
- flux_remote: float32 [4, 56, 56], replicated, may hold values from -0.75 to 0.75
- star_matrix: float32 [3, 9, 9, 20480], P(None, None, None, ('grp', 'dom')), may hold values from -0.18 to 0.18
- face_local: float32 [4, 9, 9, 20480], P(None, None, None, ('grp', 'dom')), may hold values from -0.15 to 0.15
- face_remote: float32 [4, 9, 9, 20480], P(None, None, None, ('grp', 'dom')), may hold values from -0.15 to 0.15
- energy_weight: float32 [9, 20480], P(None, ('grp', 'dom')), may hold values from 0.5 to 18
- face_neighbour: int32 [4, 20480], P(None, ('grp', 'dom')), may hold values from 0 to 1151, as said below
- element_count: int32 [32], P(('grp', 'dom')), may hold values from 160 to 640, as said below
- send_count: int32 [32, 8], P(('grp', 'dom')), may hold values from 0 to 64, as said below
- send_element: int32 [32, 8, 64], P(('grp', 'dom')), may hold values from 0 to 639, as said below
- receiver_element: int32 [512], P(('grp', 'dom')), may hold values from 0 to 639, as said below
- receiver_slot: int32 [512], P(('grp', 'dom')), may hold values from 0 to 127, as said below
- receiver_weight: float32 [56, 512], P(None, ('grp', 'dom')), may hold values from -0.75 to 0.75
Outputs:
- new_state: float32 [56, 9, 20480], P(None, None, ('grp', 'dom'))
- energy: float32 [4, 3], P('grp')
- traces: float32 [3, 9, 512], P(None, None, ('grp', 'dom'))
Inputs may be any that keep to these rules, and one draw needn't show every extreme that they name: The first element_count[p] slots of a partition are active. In every slab 4 partitions in a row along dom (cyclically) hold 640 active elements; the others hold from 160 to 320. `send_count`: every partition has exactly 64 in one of its first 6 slots. `send_element`: names active elements of the sending partition. `face_neighbour`: values below 640 name active elements of the partition itself. `receiver_element`: names an active element of the owning partition. `receiver_slot`: within each slab a permutation of the 128 rows.
All inputs are finite; a program needn't handle non-finite values.
Results may differ from a plain program's by a relative error of at most 0.0001.
Values sent between devices are 32-bit elements; how exact they have to be, the bound alone decides.
A program may use at most 128 MiB of HBM per device.

v0:
```python
import jax
import jax.numpy as jnp
from jax import lax
from jax.sharding import PartitionSpec as P

PEER_REACH = 3
TIME_STEPS = 3
highest = lax.Precision.HIGHEST


def from_behind(array, axis, by):
    count = lax.axis_size(axis)
    return lax.ppermute(array, axis, [(i, (i + by) % count) for i in range(count)])


def from_behind_2(value, axis, steps):
    count = lax.axis_size(axis)
    initial, last = (max(0, -steps), min(count, count - steps))
    return lax.ppermute(value, axis, [(source, source + steps) for source in range(initial, last)])


def element_slice(array, start, width):
    return lax.dynamic_slice_in_dim(array, start, width, array.ndim - 1)


def quantity_apply(matrices, modal_terms):
    total = None
    for column in range(matrices.shape[2]):
        term = jnp.sum(
            modal_terms[:, :, column : column + 1, :] * matrices[:, None, :, column, :], axis=0
        )
        total = term if total is None else total + term
    return total


def per_device(
    element_state,
    stiffness,
    flux_local,
    flux_remote,
    star_matrix,
    face_local,
    face_remote,
    energy_weight,
    face_neighbour,
    element_count,
    send_count,
    send_element,
    receiver_element,
    receiver_slot,
    receiver_weight,
):
    basis, quantities, elem_pad = element_state.shape
    slot_total = send_element.shape[1]
    capacity = send_element.shape[2]
    group_size = lax.axis_size("dom")
    width = min(128, elem_pad)
    live_count = element_count[0]
    live_blocks = (live_count + width - 1) // width
    stacked_local = jnp.concatenate([stiffness, flux_local], 0).reshape(-1, basis)
    local_total = stiffness.shape[0] + flux_local.shape[0]
    slot_live = jnp.arange(capacity)[None, :] < send_count[0][:, None]
    element_live = jnp.arange(elem_pad) < live_count
    denominator = float(group_size * elem_pad * basis * quantities)
    matches = (
        receiver_slot[:, None] == jnp.arange(group_size * receiver_slot.shape[0])[None, :]
    ).astype(jnp.float32)
    fields = element_state
    energies = []
    tables = []
    for time_step in range(TIME_STEPS):
        taken = jnp.take(fields, send_element[0], axis=2)
        messages = jnp.where(slot_live[None, None], taken, 0.0)

        def local_terms(block_number, partial_value):
            start = block_number * width
            block_field = element_slice(fields, start, width)
            modal_terms = jnp.dot(
                stacked_local,
                block_field.reshape(basis, -1),
                precision=highest,
                preferred_element_type=jnp.float32,
            ).reshape(local_total, basis, quantities, width)
            matrices = jnp.concatenate(
                [
                    element_slice(star_matrix, start, width),
                    -element_slice(face_local, start, width),
                ],
                0,
            )
            return lax.dynamic_update_slice_in_dim(
                partial_value, quantity_apply(matrices, modal_terms), start, 2
            )

        partial_value = lax.fori_loop(0, live_blocks, local_terms, jnp.zeros_like(fields))
        arrived = []
        for slot_number in range(2 * PEER_REACH):
            offset = slot_number + 1 if slot_number < PEER_REACH else PEER_REACH - 1 - slot_number
            arrived.append(from_behind(messages[:, :, slot_number, :], "dom", offset))
        for slot_number in range(2 * PEER_REACH, 2 * PEER_REACH + 2):
            offset = 1 if slot_number == 2 * PEER_REACH else -1
            arrived.append(from_behind_2(messages[:, :, slot_number, :], "grp", offset))
        halo_cells = jnp.stack(arrived, 2).reshape(basis, quantities, slot_total * capacity)
        extended = jnp.concatenate([fields, halo_cells], 2)

        def remote_terms(block_number, updated):
            start = block_number * width
            block_field = element_slice(fields, start, width)
            neighbours = element_slice(face_neighbour, start, width)
            nearby = jnp.take(extended, neighbours, axis=2)
            modal_terms = jnp.einsum("fbc,cqfe->fbqe", flux_remote, nearby, precision=highest)
            change = element_slice(partial_value, start, width) - quantity_apply(
                element_slice(face_remote, start, width), modal_terms
            )
            live = start + jnp.arange(width) < live_count
            renewed = jnp.where(live[None, None, :], block_field + change, block_field)
            return lax.dynamic_update_slice_in_dim(updated, renewed, start, 2)

        fields = lax.fori_loop(0, live_blocks, remote_terms, fields)
        squares = jnp.sum(fields * fields, axis=0)
        own_energy = 0.5 * jnp.sum(jnp.where(element_live[None, :], energy_weight * squares, 0.0))
        energies.append(lax.psum(own_energy, "dom") / denominator)
        values = jnp.einsum(
            "br,bqr->qr",
            receiver_weight,
            jnp.take(fields, receiver_element, axis=2),
            precision=highest,
        )
        placed = jnp.dot(values, matches, precision=highest, preferred_element_type=jnp.float32)
        tables.append(placed)
    energy = jnp.stack(energies)
    traces = lax.psum_scatter(jnp.stack(tables), "dom", scatter_dimension=2, tiled=True)
    return (fields, energy[None, :], traces)


def solution(mesh):
    return jax.shard_map(
        per_device,
        mesh=mesh,
        in_specs=(
            P(None, None, ("grp", "dom")),
            P(),
            P(),
            P(),
            P(None, None, None, ("grp", "dom")),
            P(None, None, None, ("grp", "dom")),
            P(None, None, None, ("grp", "dom")),
            P(None, ("grp", "dom")),
            P(None, ("grp", "dom")),
            P(("grp", "dom")),
            P(("grp", "dom"), None),
            P(("grp", "dom"), None, None),
            P(("grp", "dom")),
            P(("grp", "dom")),
            P(None, ("grp", "dom")),
        ),
        out_specs=(P(None, None, ("grp", "dom")), P("grp", None), P(None, None, ("grp", "dom"))),
        check_vma=False,
    )
```

profile of v0, /device:TPU:0, one launch (start us, length us, event | category | flops | bytes accessed | tf_op | source)
XLA Modules:
  0.0 804.4 jit_solution(14370141529047191707)
XLA Ops:
  40.7 36.1 %while.60 = (s32[]{:T(128)}, f32[56,9,640]{2,0,1:T(8,128)}, s32[]{:T(128)}, f32[56,9,640]{2,0,1:T(8,128)}, f32[392,56]{1,0:T(8,128)S(1)}, /*index=5*/f32[3,9,9,6...) while((s32[]{:T(128)}, f32[56,9,640]{2,0,1:T(8,128)}, ...), condition=%wide.region_10.12_spmd, body=%wide.region_0.11_spmd.sunk | while | flops 311642496 | bytes 30054112 | solution.py:95
  82.7 29.6 %collective-permute-done.1 = f32[56,9,64]{2,0,1:T(8,128)S(1)} collective-permute-done((f32[56,9,64]{2,0,1:T(8,128)S(1)}, f32[56,9,64]{2,0,1:T(8,128)S(1)}, u32[]{:S(2)}, u32[]{:S(2)}) %collective-permute-start.1) | collective-permute-done | bytes 129056 | tf_op jit(solution)/shard_map/ppermute | solution.py:13
  112.9 14.0 %collective-permute-done.2 = f32[56,9,64]{2,0,1:T(8,128)S(1)} collective-permute-done((f32[56,9,64]{2,0,1:T(8,128)S(1)}, f32[56,9,64]{2,0,1:T(8,128)S(1)}, u32[]{:S(2)}, u32[]{:S(2)}) %collective-permute-start.2) | collective-permute-done | bytes 129056 | tf_op jit(solution)/shard_map/ppermute | solution.py:13
  126.9 6.7 collective-permute-done.3
  144.1 8.3 %copy.285 = f32[56,9,1152]{0,1,2:T(8,128)} copy(f32[56,9,1152]{2,0,1:T(8,128)} %pad_maximum_fusion.3) | data formatting | bytes 4644864 | tf_op jit(solution)/shard_map/while | solution.py:119
  152.4 51.5 %while.61 = (s32[]{:T(128)}, f32[56,9,640]{2,0,1:T(8,128)S(1)}, s32[]{:T(128)}, s32[]{:T(128)}, f32[56,9,640]{2,0,1:T(8,128)}, /*index=5*/f32[56,9,640]{2,0,1:T(...) while((s32[]{:T(128)}, f32[56,9,640]{2,0,1:T(8,128)S(1)}, ...), condition=%wide.region_21.24_spmd, body=%wide.region_11.23_spmd.sunk | while | flops 178446096 | bytes 18001700 | solution.py:119
  155.7 6.7 gather_fusion
  172.7 6.7 gather_fusion
  189.7 6.7 gather_fusion
  211.6 36.2 %while.62 = (s32[]{:T(128)}, f32[56,9,640]{2,0,1:T(8,128)}, s32[]{:T(128)}, f32[56,9,640]{2,0,1:T(8,128)S(1)}, f32[392,56]{1,0:T(8,128)S(1)}, /*index=5*/f32[3,9...) while((s32[]{:T(128)}, f32[56,9,640]{2,0,1:T(8,128)}, ...), condition=%wide.region_32.35_spmd, body=%wide.region_22.34_spmd.sunk | while | flops 311642496 | bytes 29134816 | solution.py:95
  266.9 60.5 %collective-permute-start.13 = (f32[56,9,64]{2,0,1:T(8,128)S(1)}, f32[56,9,64]{2,0,1:T(8,128)S(1)}, u32[]{:S(2)}, u32[]{:S(2)}) collective-permute-start(f32[56,9,64]{2,0,1:T(8,128)S(1)} %get-tuple-element.754), channel_id=1, source_target_pairs={{0,5},{1,6},{2,7},{3,0},{4,1},{5,2},{6,3},{7,4},{8,13},{9,14},{10,... | collective-permute-start | bytes 387080 | tf_op jit(solution)/shard_map/ppermute | solution.py:13
  330.4 15.6 %collective-permute-done.8 = f32[56,9,64]{2,0,1:T(8,128)S(1)} collective-permute-done((f32[56,9,64]{2,0,1:T(8,128)S(1)}, f32[56,9,64]{2,0,1:T(8,128)S(1)}, u32[]{:S(2)}, u32[]{:S(2)}) %collective-permute-start.8) | collective-permute-done | bytes 129056 | tf_op jit(solution)/shard_map/ppermute | solution.py:13
  347.9 8.2 %collective-permute-done.9 = f32[56,9,64]{2,0,1:T(8,128)S(1)} collective-permute-done((f32[56,9,64]{2,0,1:T(8,128)S(1)}, f32[56,9,64]{2,0,1:T(8,128)S(1)}, u32[]{:S(2)}, u32[]{:S(2)}) %collective-permute-start.9) | collective-permute-done | bytes 129056 | tf_op jit(solution)/shard_map/ppermute | solution.py:13
  356.1 13.0 %collective-permute-done.10 = f32[56,9,64]{2,0,1:T(8,128)S(1)} collective-permute-done((f32[56,9,64]{2,0,1:T(8,128)S(1)}, f32[56,9,64]{2,0,1:T(8,128)S(1)}, u32[]{:S(2)}, u32[]{:S(2)}) %collective-permute-start.10) | collective-permute-done | bytes 129056 | tf_op jit(solution)/shard_map/ppermute | solution.py:13
  369.3 8.1 %collective-permute-done.11 = f32[56,9,64]{2,0,1:T(8,128)S(1)} collective-permute-done((f32[56,9,64]{2,0,1:T(8,128)S(1)}, f32[56,9,64]{2,0,1:T(8,128)S(1)}, u32[]{:S(2)}, u32[]{:S(2)}) %collective-permute-start.11) | collective-permute-done | bytes 129056 | tf_op jit(solution)/shard_map/ppermute | solution.py:13
  382.7 8.4 %copy.293 = f32[56,9,1152]{0,1,2:T(8,128)} copy(f32[56,9,1152]{2,0,1:T(8,128)} %pad_maximum_fusion.4) | data formatting | bytes 4644864 | tf_op jit(solution)/shard_map/while | solution.py:119
  391.1 51.0 %while.63 = (s32[]{:T(128)}, f32[56,9,640]{2,0,1:T(8,128)S(1)}, s32[]{:T(128)}, s32[]{:T(128)}, f32[56,9,640]{2,0,1:T(8,128)}, /*index=5*/f32[56,9,640]{2,0,1:T(...) while((s32[]{:T(128)}, f32[56,9,640]{2,0,1:T(8,128)S(1)}, ...), condition=%wide.region_43.46_spmd, body=%wide.region_33.45_spmd.sunk | while | flops 178446096 | bytes 18001700 | solution.py:119
  394.0 6.7 gather_fusion.1
  411.0 6.7 gather_fusion.1
  428.0 6.7 gather_fusion.1
  457.3 36.4 %while.64 = (s32[]{:T(128)}, f32[56,9,640]{2,0,1:T(8,128)}, s32[]{:T(128)}, f32[56,9,640]{2,0,1:T(8,128)S(1)}, f32[392,56]{1,0:T(8,128)S(1)}, /*index=5*/f32[3,9...) while((s32[]{:T(128)}, f32[56,9,640]{2,0,1:T(8,128)}, ...), condition=%wide.region_54.57_spmd, body=%wide.region_44.56_spmd.sunk | while | flops 311642496 | bytes 29134816 | solution.py:95
  506.3 61.6 %collective-permute-start.21 = (f32[56,9,64]{2,0,1:T(8,128)S(1)}, f32[56,9,64]{2,0,1:T(8,128)S(1)}, u32[]{:S(2)}, u32[]{:S(2)}) collective-permute-start(f32[56,9,64]{2,0,1:T(8,128)S(1)} %get-tuple-element.746), channel_id=1, source_target_pairs={{0,5},{1,6},{2,7},{3,0},{4,1},{5,2},{6,3},{7,4},{8,13},{9,14},{10,... | collective-permute-start | bytes 387080 | tf_op jit(solution)/shard_map/ppermute | solution.py:13
  570.2 15.8 %collective-permute-done.17 = f32[56,9,64]{2,0,1:T(8,128)S(1)} collective-permute-done((f32[56,9,64]{2,0,1:T(8,128)S(1)}, f32[56,9,64]{2,0,1:T(8,128)S(1)}, u32[]{:S(2)}, u32[]{:S(2)}) %collective-permute-start.17) | collective-permute-done | bytes 129056 | tf_op jit(solution)/shard_map/ppermute | solution.py:13
  588.6 12.8 %collective-permute-done.18 = f32[56,9,64]{2,0,1:T(8,128)S(1)} collective-permute-done((f32[56,9,64]{2,0,1:T(8,128)S(1)}, f32[56,9,64]{2,0,1:T(8,128)S(1)}, u32[]{:S(2)}, u32[]{:S(2)}) %collective-permute-start.18) | collective-permute-done | bytes 129056 | tf_op jit(solution)/shard_map/ppermute | solution.py:13
  601.4 7.1 collective-permute-done.19
  613.8 8.3 %copy.307 = f32[56,9,1152]{0,1,2:T(8,128)} copy(f32[56,9,1152]{2,0,1:T(8,128)} %pad_maximum_fusion.5) | data formatting | bytes 4644864 | tf_op jit(solution)/shard_map/while | solution.py:119
  622.1 47.4 %while.65 = (s32[]{:T(128)}, f32[56,9,640]{2,0,1:T(8,128)}, s32[]{:T(128)}, s32[]{:T(128)}, f32[56,9,640]{2,0,1:T(8,128)S(1)}, /*index=5*/f32[56,9,640]{2,0,1:T(...) while((s32[]{:T(128)}, f32[56,9,640]{2,0,1:T(8,128)}, ...), condition=%wide.region_65.68_spmd, body=%wide.region_55.67_spmd.sunk | while | flops 178446096 | bytes 17336972 | solution.py:119
  623.8 6.7 gather_fusion.2
  639.6 6.7 gather_fusion.2
  655.4 6.7 gather_fusion.2
  678.5 52.2 %all-reduce = (f32[]{:T(128)}, f32[]{:T(128)}, f32[]{:T(128)}) all-reduce(f32[]{:T(128)S(6)} %mul.971, f32[]{:T(128)S(6)} %mul.968, f32[]{:T(128)S(6)} %mul.965), channel_id=1, replica_groups=mesh['grp'=4,'dom'=8] {'dom'}, use_global_device_ids=true, to_apply=%region_74.77 | all-reduce | flops 3 | bytes 24 | tf_op jit(solution)/shard_map/psum | solution.py:122
  738.0 57.9 %reduce-scatter.4.cloned.1.call-done = f32[16,27]{1,0:T(8,128)} async-done(((f32[128,27]{1,0:T(8,128)}), f32[16,27]{1,0:T(8,128)}) %reduce-scatter.4.cloned.1.call-update) | async-done | bytes 1744
  (740 shorter events, 332.3 us)
Async XLA Ops:
  7.2 322.0 %copy-start = (f32[56,16]{0,1:T(8,128)S(1)}, f32[56,16]{0,1:T(8,128)}, u32[]{:S(2)}) copy-start(f32[56,16]{0,1:T(8,128)} %param.47) | copy-start | bytes 10756
  7.2 788.7 %reduce-scatter.4.cloned.1.call-start = ((), (), s32[]{:S(2)}) async-start(), calls=%async_computation.1 | async-start | bytes 73728
  25.4 111.2 %collective-permute-start.7 = (f32[56,9,64]{2,0,1:T(8,128)}, f32[56,9,64]{2,0,1:T(8,128)}, u32[]{:S(2)}, u32[]{:S(2)}) collective-permute-start(f32[56,9,64]{2,0,1:T(8,128)} %get-tuple-element.760), channel_id=1, source_target_pairs={{8,0},{16,8},{24,16},{9,1},{17,9},{25,17},{10,2},{18,10},{26,18},{... | collective-permute-start | bytes 387080 | tf_op jit(solution)/shard_map/ppermute | solution.py:19
  26.7 109.0 %collective-permute-start.6 = (f32[56,9,64]{2,0,1:T(8,128)}, f32[56,9,64]{2,0,1:T(8,128)}, u32[]{:S(2)}, u32[]{:S(2)}) collective-permute-start(f32[56,9,64]{2,0,1:T(8,128)} %get-tuple-element.761), channel_id=1, source_target_pairs={{0,8},{8,16},{16,24},{1,9},{9,17},{17,25},{2,10},{10,18},{18,26},{... | collective-permute-start | bytes 387080 | tf_op jit(solution)/shard_map/ppermute | solution.py:19
  30.4 104.2 %collective-permute-start.5 = (f32[56,9,64]{2,0,1:T(8,128)}, f32[56,9,64]{2,0,1:T(8,128)}, u32[]{:S(2)}, u32[]{:S(2)}) collective-permute-start(f32[56,9,64]{2,0,1:T(8,128)} %get-tuple-element.762), channel_id=1, source_target_pairs={{0,5},{1,6},{2,7},{3,0},{4,1},{5,2},{6,3},{7,4},{8,13},{9,14},{10,... | collective-permute-start | bytes 387080 | tf_op jit(solution)/shard_map/ppermute | solution.py:13
  35.4 98.3 %collective-permute-start.4 = (f32[56,9,64]{2,0,1:T(8,128)}, f32[56,9,64]{2,0,1:T(8,128)}, u32[]{:S(2)}, u32[]{:S(2)}) collective-permute-start(f32[56,9,64]{2,0,1:T(8,128)} %get-tuple-element.763), channel_id=1, source_target_pairs={{0,6},{1,7},{2,0},{3,1},{4,2},{5,3},{6,4},{7,5},{8,14},{9,15},{10,... | collective-permute-start | bytes 387080 | tf_op jit(solution)/shard_map/ppermute | solution.py:13
  36.8 44.9 %collective-permute-start = (f32[56,9,64]{2,0,1:T(8,128)}, f32[56,9,64]{2,0,1:T(8,128)}, u32[]{:S(2)}, u32[]{:S(2)}) collective-permute-start(f32[56,9,64]{2,0,1:T(8,128)} %get-tuple-element.767), channel_id=1, source_target_pairs={{0,1},{1,2},{2,3},{3,4},{4,5},{5,6},{6,7},{7,0},{8,9},{9,10},{10,1... | collective-permute-start | bytes 387080 | tf_op jit(solution)/shard_map/ppermute | solution.py:13
  81.7 30.5 %collective-permute-start.1 = (f32[56,9,64]{2,0,1:T(8,128)S(1)}, f32[56,9,64]{2,0,1:T(8,128)S(1)}, u32[]{:S(2)}, u32[]{:S(2)}) collective-permute-start(f32[56,9,64]{2,0,1:T(8,128)S(1)} %copy-done.63), channel_id=1, source_target_pairs={{0,2},{1,3},{2,4},{3,5},{4,6},{5,7},{6,0},{7,1},{8,10},{9,11},{10,... | collective-permute-start | bytes 387080 | tf_op jit(solution)/shard_map/ppermute | solution.py:13
  112.2 14.7 %collective-permute-start.2 = (f32[56,9,64]{2,0,1:T(8,128)S(1)}, f32[56,9,64]{2,0,1:T(8,128)S(1)}, u32[]{:S(2)}, u32[]{:S(2)}) collective-permute-start(f32[56,9,64]{2,0,1:T(8,128)S(1)} %copy-done.62), channel_id=1, source_target_pairs={{0,3},{1,4},{2,5},{3,6},{4,7},{5,0},{6,1},{7,2},{8,11},{9,12},{10,... | collective-permute-start | bytes 387080 | tf_op jit(solution)/shard_map/ppermute | solution.py:13
  126.9 6.7 collective-permute-start.3
  247.8 133.4 %copy-start.6 = (f32[56,9,640]{2,0,1:T(8,128)}, f32[56,9,640]{2,0,1:T(8,128)S(1)}, u32[]{:S(2)}) copy-start(f32[56,9,640]{2,0,1:T(8,128)S(1)} %get-tuple-element.1701) | copy-start | bytes 3870724
  262.4 66.8 %copy-start.74 = (pred[16]{0:T(512)(128)(4,1)S(1)}, pred[16]{0:T(512)(128)(4,1)}, u32[]{:S(2)}) copy-start(pred[16]{0:T(512)(128)(4,1)} %compare_and_fusion.4) | copy-start | bytes 52
  262.4 67.2 %copy-start.79 = (s32[16]{0:T(128)S(1)}, s32[16]{0:T(128)}, u32[]{:S(2)}) copy-start(s32[16]{0:T(128)} %param.46) | copy-start | bytes 196
  262.5 115.0 %collective-permute-start.15 = (f32[56,9,64]{2,0,1:T(8,128)S(1)}, f32[56,9,64]{2,0,1:T(8,128)S(1)}, u32[]{:S(2)}, u32[]{:S(2)}) collective-permute-start(f32[56,9,64]{2,0,1:T(8,128)S(1)} %get-tuple-element.752), channel_id=1, source_target_pairs={{8,0},{16,8},{24,16},{9,1},{17,9},{25,17},{10,2},{18,10},{26,18},{... | collective-permute-start | bytes 387080 | tf_op jit(solution)/shard_map/ppermute | solution.py:19
  263.8 113.6 %collective-permute-start.14 = (f32[56,9,64]{2,0,1:T(8,128)S(1)}, f32[56,9,64]{2,0,1:T(8,128)S(1)}, u32[]{:S(2)}, u32[]{:S(2)}) collective-permute-start(f32[56,9,64]{2,0,1:T(8,128)S(1)} %get-tuple-element.753), channel_id=1, source_target_pairs={{0,8},{8,16},{16,24},{1,9},{9,17},{17,25},{2,10},{10,18},{18,26},{... | collective-permute-start | bytes 387080 | tf_op jit(solution)/shard_map/ppermute | solution.py:19
  266.9 110.5 %collective-permute-start.13 = (f32[56,9,64]{2,0,1:T(8,128)S(1)}, f32[56,9,64]{2,0,1:T(8,128)S(1)}, u32[]{:S(2)}, u32[]{:S(2)}) collective-permute-start(f32[56,9,64]{2,0,1:T(8,128)S(1)} %get-tuple-element.754), channel_id=1, source_target_pairs={{0,5},{1,6},{2,7},{3,0},{4,1},{5,2},{6,3},{7,4},{8,13},{9,14},{10,... | collective-permute-start | bytes 387080 | tf_op jit(solution)/shard_map/ppermute | solution.py:13
  327.4 50.0 %collective-permute-start.12 = (f32[56,9,64]{2,0,1:T(8,128)S(1)}, f32[56,9,64]{2,0,1:T(8,128)S(1)}, u32[]{:S(2)}, u32[]{:S(2)}) collective-permute-start(f32[56,9,64]{2,0,1:T(8,128)S(1)} %get-tuple-element.755), channel_id=1, source_target_pairs={{0,6},{1,7},{2,0},{3,1},{4,2},{5,3},{6,4},{7,5},{8,14},{9,15},{10,... | collective-permute-start | bytes 387080 | tf_op jit(solution)/shard_map/ppermute | solution.py:13
  327.8 18.2 %collective-permute-start.8 = (f32[56,9,64]{2,0,1:T(8,128)S(1)}, f32[56,9,64]{2,0,1:T(8,128)S(1)}, u32[]{:S(2)}, u32[]{:S(2)}) collective-permute-start(f32[56,9,64]{2,0,1:T(8,128)S(1)} %get-tuple-element.759), channel_id=1, source_target_pairs={{0,1},{1,2},{2,3},{3,4},{4,5},{5,6},{6,7},{7,0},{8,9},{9,10},{10,1... | collective-permute-start | bytes 387080 | tf_op jit(solution)/shard_map/ppermute | solution.py:13
  346.0 10.0 %collective-permute-start.9 = (f32[56,9,64]{2,0,1:T(8,128)S(1)}, f32[56,9,64]{2,0,1:T(8,128)S(1)}, u32[]{:S(2)}, u32[]{:S(2)}) collective-permute-start(f32[56,9,64]{2,0,1:T(8,128)S(1)} %get-tuple-element.758), channel_id=1, source_target_pairs={{0,2},{1,3},{2,4},{3,5},{4,6},{5,7},{6,0},{7,1},{8,10},{9,11},{10,... | collective-permute-start | bytes 387080 | tf_op jit(solution)/shard_map/ppermute | solution.py:13
  356.0 13.0 %collective-permute-start.10 = (f32[56,9,64]{2,0,1:T(8,128)S(1)}, f32[56,9,64]{2,0,1:T(8,128)S(1)}, u32[]{:S(2)}, u32[]{:S(2)}) collective-permute-start(f32[56,9,64]{2,0,1:T(8,128)S(1)} %get-tuple-element.757), channel_id=1, source_target_pairs={{0,3},{1,4},{2,5},{3,6},{4,7},{5,0},{6,1},{7,2},{8,11},{9,12},{10,... | collective-permute-start | bytes 387080 | tf_op jit(solution)/shard_map/ppermute | solution.py:13
  369.1 8.3 %collective-permute-start.11 = (f32[56,9,64]{2,0,1:T(8,128)S(1)}, f32[56,9,64]{2,0,1:T(8,128)S(1)}, u32[]{:S(2)}, u32[]{:S(2)}) collective-permute-start(f32[56,9,64]{2,0,1:T(8,128)S(1)} %get-tuple-element.756), channel_id=1, source_target_pairs={{0,7},{1,0},{2,1},{3,2},{4,3},{5,4},{6,5},{7,6},{8,15},{9,8},{10,9... | collective-permute-start | bytes 387080 | tf_op jit(solution)/shard_map/ppermute | solution.py:13
  500.7 67.4 %copy-start.80 = (s32[16]{0:T(128)S(1)}, s32[16]{0:T(128)}, u32[]{:S(2)}) copy-start(s32[16]{0:T(128)} %param.46) | copy-start | bytes 196
  500.7 67.6 %collective-permute-start.16 = (f32[56,9,64]{2,0,1:T(8,128)S(1)}, f32[56,9,64]{2,0,1:T(8,128)S(1)}, u32[]{:S(2)}, u32[]{:S(2)}) collective-permute-start(f32[56,9,64]{2,0,1:T(8,128)S(1)} %get-tuple-element.751), channel_id=1, source_target_pairs={{0,1},{1,2},{2,3},{3,4},{4,5},{5,6},{6,7},{7,0},{8,9},{9,10},{10,1... | collective-permute-start | bytes 387080 | tf_op jit(solution)/shard_map/ppermute | solution.py:13
  501.9 106.7 %collective-permute-start.23 = (f32[56,9,64]{2,0,1:T(8,128)S(1)}, f32[56,9,64]{2,0,1:T(8,128)S(1)}, u32[]{:S(2)}, u32[]{:S(2)}) collective-permute-start(f32[56,9,64]{2,0,1:T(8,128)S(1)} %get-tuple-element.744), channel_id=1, source_target_pairs={{8,0},{16,8},{24,16},{9,1},{17,9},{25,17},{10,2},{18,10},{26,18},{... | collective-permute-start | bytes 387080 | tf_op jit(solution)/shard_map/ppermute | solution.py:19
  503.2 105.4 %collective-permute-start.22 = (f32[56,9,64]{2,0,1:T(8,128)S(1)}, f32[56,9,64]{2,0,1:T(8,128)S(1)}, u32[]{:S(2)}, u32[]{:S(2)}) collective-permute-start(f32[56,9,64]{2,0,1:T(8,128)S(1)} %get-tuple-element.745), channel_id=1, source_target_pairs={{0,8},{8,16},{16,24},{1,9},{9,17},{17,25},{2,10},{10,18},{18,26},{... | collective-permute-start | bytes 387080 | tf_op jit(solution)/shard_map/ppermute | solution.py:19
  506.3 102.3 %collective-permute-start.21 = (f32[56,9,64]{2,0,1:T(8,128)S(1)}, f32[56,9,64]{2,0,1:T(8,128)S(1)}, u32[]{:S(2)}, u32[]{:S(2)}) collective-permute-start(f32[56,9,64]{2,0,1:T(8,128)S(1)} %get-tuple-element.746), channel_id=1, source_target_pairs={{0,5},{1,6},{2,7},{3,0},{4,1},{5,2},{6,3},{7,4},{8,13},{9,14},{10,... | collective-permute-start | bytes 387080 | tf_op jit(solution)/shard_map/ppermute | solution.py:13
  567.9 40.6 %collective-permute-start.20 = (f32[56,9,64]{2,0,1:T(8,128)S(1)}, f32[56,9,64]{2,0,1:T(8,128)S(1)}, u32[]{:S(2)}, u32[]{:S(2)}) collective-permute-start(f32[56,9,64]{2,0,1:T(8,128)S(1)} %get-tuple-element.747), channel_id=1, source_target_pairs={{0,6},{1,7},{2,0},{3,1},{4,2},{5,3},{6,4},{7,5},{8,14},{9,15},{10,... | collective-permute-start | bytes 387080 | tf_op jit(solution)/shard_map/ppermute | solution.py:13
  568.3 17.7 %collective-permute-start.17 = (f32[56,9,64]{2,0,1:T(8,128)S(1)}, f32[56,9,64]{2,0,1:T(8,128)S(1)}, u32[]{:S(2)}, u32[]{:S(2)}) collective-permute-start(f32[56,9,64]{2,0,1:T(8,128)S(1)} %get-tuple-element.750), channel_id=1, source_target_pairs={{0,2},{1,3},{2,4},{3,5},{4,6},{5,7},{6,0},{7,1},{8,10},{9,11},{10,... | collective-permute-start | bytes 387080 | tf_op jit(solution)/shard_map/ppermute | solution.py:13
  586.0 15.3 %collective-permute-start.18 = (f32[56,9,64]{2,0,1:T(8,128)S(1)}, f32[56,9,64]{2,0,1:T(8,128)S(1)}, u32[]{:S(2)}, u32[]{:S(2)}) collective-permute-start(f32[56,9,64]{2,0,1:T(8,128)S(1)} %get-tuple-element.749), channel_id=1, source_target_pairs={{0,3},{1,4},{2,5},{3,6},{4,7},{5,0},{6,1},{7,2},{8,11},{9,12},{10,... | collective-permute-start | bytes 387080 | tf_op jit(solution)/shard_map/ppermute | solution.py:13
  601.3 7.1 collective-permute-start.19
  673.7 62.1 %copy-start.76 = (pred[16]{0:T(512)(128)(4,1)S(1)}, pred[16]{0:T(512)(128)(4,1)}, u32[]{:S(2)}) copy-start(pred[16]{0:T(512)(128)(4,1)} %compare_and_fusion.4) | copy-start | bytes 52
  673.7 62.7 %copy-start.73 = (f32[1,9,128]{2,1,0:T(8,128)S(1)}, f32[1,9,128]{2,1,0:T(8,128)}, u32[]{:S(2)}) copy-start(f32[1,9,128]{2,1,0:T(8,128)} %convolution_bitcast_fusion.8) | copy-start | bytes 13828
  (180 other events, 578.2 us)
Sparse Core Ops, SparseCore 0:
  737.5 58.3 reduce-scatter.3
where the time goes:
time: 819 us; the launch traced here: 804 us
  local copies, waits for them, and re-layouts  262 us (32%)
  waiting for transfers between devices  189 us (23%)
  starting transfers between devices  152 us (19%)
  other arithmetic  83.2 us (10%)
  blocking collectives  52.2 us (6%)
  matrix products  42.8 us (5%)
  between operations  19.4 us (2%)
    ppermute x18, starting transfers between devices, from_behind(): lax.ppermute(array, axis, [(i, (i + by) % count) for i in range(count)])  138 us
    ppermute x18, waiting for transfers between devices, from_behind(): lax.ppermute(array, axis, [(i, (i + by) % count) for i in range(count)])  131 us
    gather x18, local copies, waits for them, and re-layouts, remote_terms(): nearby = jnp.take(extended, neighbours, axis=2)  90.2 us
    unnamed x2, waiting for transfers between devices  57.9 us
    psum x1, blocking collectives, per_device(): energies.append(lax.psum(own_energy, 'dom') / denominator)  52.2 us
    while x7, local copies, waits for them, and re-layouts, per_device(): fields = lax.fori_loop(0, live_blocks, remote_terms, fields)  40.5 us
    dot_general x9, matrix products, local_terms(): jnp.dot(stacked_local, block_field.reshape(basis, -1), precision=highest,...  29.6 us
    gather x6, local copies, waits for them, and re-layouts, per_device(): taken = jnp.take(fields, send_element[0], axis=2)  26.9 us
  transfers between devices with their start and end apart: 25, of which 11 were waited for; matrix products, arithmetic and copies ran while one was open for 6% of the time, Pallas kernels for 0%

commit v1 on v0

--- a/solution.py
+++ b/solution.py
@@ -119,7 +119,7 @@
         fields = lax.fori_loop(0, live_blocks, remote_terms, fields)
         squares = jnp.sum(fields * fields, axis=0)
         own_energy = 0.5 * jnp.sum(jnp.where(element_live[None, :], energy_weight * squares, 0.0))
-        energies.append(lax.psum(own_energy, "dom") / denominator)
+        energies.append(jnp.sum(lax.all_gather(own_energy, "dom"), axis=0) / denominator)
         values = jnp.einsum(
             "br,bqr->qr",
             receiver_weight,

time: 819 us -> 823 us (level)
    psum x1 -> x0, blocking collectives: 52.2 us -> none  [per_device(): energies.append(lax.psum(own_energy, 'dom') / denominator)]
    unnamed x0 -> x1, blocking collectives: none -> 51.6 us
    unnamed x85 -> x94, local copies, waits for them, and re-layouts: 16.9 us -> 19.5 us
where the time goes in v1:
time: 823 us; the launch traced here: 808 us
  local copies, waits for them, and re-layouts  265 us (32%)
  waiting for transfers between devices  189 us (23%)
  starting transfers between devices  152 us (18%)
  other arithmetic  85 us (10%)
  blocking collectives  51.6 us (6%)
  matrix products  42.8 us (5%)
  between operations  19.5 us (2%)
    ppermute x18, starting transfers between devices, from_behind(): lax.ppermute(array, axis, [(i, (i + by) % count) for i in range(count)])  138 us
    ppermute x18, waiting for transfers between devices, from_behind(): lax.ppermute(array, axis, [(i, (i + by) % count) for i in range(count)])  131 us
    gather x18, local copies, waits for them, and re-layouts, remote_terms(): nearby = jnp.take(extended, neighbours, axis=2)  90.2 us
    unnamed x2, waiting for transfers between devices  57.9 us
    unnamed x1, blocking collectives  51.6 us
    while x7, local copies, waits for them, and re-layouts, per_device(): fields = lax.fori_loop(0, live_blocks, remote_terms, fields)  40.5 us
    dot_general x9, matrix products, local_terms(): jnp.dot(stacked_local, block_field.reshape(basis, -1), precision=highest,...  29.6 us
    gather x6, local copies, waits for them, and re-layouts, per_device(): taken = jnp.take(fields, send_element[0], axis=2)  26.9 us
  transfers between devices with their start and end apart: 25, of which 11 were waited for; matrix products, arithmetic and copies ran while one was open for 6% of the time, Pallas kernels for 0%

profile of v1, /device:TPU:0, one launch (start us, length us, event | category | flops | bytes accessed | tf_op | source)
XLA Modules:
  0.0 808.3 jit_solution(16460552303858930530)
XLA Ops:
  40.7 36.1 %while.60 = (s32[]{:T(128)}, f32[56,9,640]{2,0,1:T(8,128)}, s32[]{:T(128)}, f32[56,9,640]{2,0,1:T(8,128)}, f32[392,56]{1,0:T(8,128)S(1)}, /*index=5*/f32[3,9,9,6...) while((s32[]{:T(128)}, f32[56,9,640]{2,0,1:T(8,128)}, ...), condition=%wide.region_10.12_spmd, body=%wide.region_0.11_spmd.sunk | while | flops 311642496 | bytes 30054112 | solution.py:95
  83.2 29.6 %collective-permute-done.1 = f32[56,9,64]{2,0,1:T(8,128)S(1)} collective-permute-done((f32[56,9,64]{2,0,1:T(8,128)S(1)}, f32[56,9,64]{2,0,1:T(8,128)S(1)}, u32[]{:S(2)}, u32[]{:S(2)}) %collective-permute-start.1) | collective-permute-done | bytes 129056 | tf_op jit(solution)/shard_map/ppermute | solution.py:13
  113.4 14.0 %collective-permute-done.2 = f32[56,9,64]{2,0,1:T(8,128)S(1)} collective-permute-done((f32[56,9,64]{2,0,1:T(8,128)S(1)}, f32[56,9,64]{2,0,1:T(8,128)S(1)}, u32[]{:S(2)}, u32[]{:S(2)}) %collective-permute-start.2) | collective-permute-done | bytes 129056 | tf_op jit(solution)/shard_map/ppermute | solution.py:13
  127.5 6.7 collective-permute-done.3
  144.6 8.3 %copy.285 = f32[56,9,1152]{0,1,2:T(8,128)} copy(f32[56,9,1152]{2,0,1:T(8,128)} %pad_maximum_fusion.3) | data formatting | bytes 4644864 | tf_op jit(solution)/shard_map/while | solution.py:119
  153.0 51.5 %while.61 = (s32[]{:T(128)}, f32[56,9,640]{2,0,1:T(8,128)S(1)}, s32[]{:T(128)}, s32[]{:T(128)}, f32[56,9,640]{2,0,1:T(8,128)}, /*index=5*/f32[56,9,640]{2,0,1:T(...) while((s32[]{:T(128)}, f32[56,9,640]{2,0,1:T(8,128)S(1)}, ...), condition=%wide.region_21.24_spmd, body=%wide.region_11.23_spmd.sunk | while | flops 178446096 | bytes 18001700 | solution.py:119
  156.3 6.7 gather_fusion
  173.3 6.7 gather_fusion
  190.3 6.7 gather_fusion
  212.1 36.3 %while.62 = (s32[]{:T(128)}, f32[56,9,640]{2,0,1:T(8,128)}, s32[]{:T(128)}, f32[56,9,640]{2,0,1:T(8,128)S(1)}, f32[392,56]{1,0:T(8,128)S(1)}, /*index=5*/f32[3,9...) while((s32[]{:T(128)}, f32[56,9,640]{2,0,1:T(8,128)}, ...), condition=%wide.region_32.35_spmd, body=%wide.region_22.34_spmd.sunk | while | flops 311642496 | bytes 29134816 | solution.py:95
  267.5 60.5 %collective-permute-start.13 = (f32[56,9,64]{2,0,1:T(8,128)S(1)}, f32[56,9,64]{2,0,1:T(8,128)S(1)}, u32[]{:S(2)}, u32[]{:S(2)}) collective-permute-start(f32[56,9,64]{2,0,1:T(8,128)S(1)} %get-tuple-element.754), channel_id=1, source_target_pairs={{0,5},{1,6},{2,7},{3,0},{4,1},{5,2},{6,3},{7,4},{8,13},{9,14},{10,... | collective-permute-start | bytes 387080 | tf_op jit(solution)/shard_map/ppermute | solution.py:13
  330.9 15.6 %collective-permute-done.8 = f32[56,9,64]{2,0,1:T(8,128)S(1)} collective-permute-done((f32[56,9,64]{2,0,1:T(8,128)S(1)}, f32[56,9,64]{2,0,1:T(8,128)S(1)}, u32[]{:S(2)}, u32[]{:S(2)}) %collective-permute-start.8) | collective-permute-done | bytes 129056 | tf_op jit(solution)/shard_map/ppermute | solution.py:13
  348.4 8.2 %collective-permute-done.9 = f32[56,9,64]{2,0,1:T(8,128)S(1)} collective-permute-done((f32[56,9,64]{2,0,1:T(8,128)S(1)}, f32[56,9,64]{2,0,1:T(8,128)S(1)}, u32[]{:S(2)}, u32[]{:S(2)}) %collective-permute-start.9) | collective-permute-done | bytes 129056 | tf_op jit(solution)/shard_map/ppermute | solution.py:13
  356.6 13.0 %collective-permute-done.10 = f32[56,9,64]{2,0,1:T(8,128)S(1)} collective-permute-done((f32[56,9,64]{2,0,1:T(8,128)S(1)}, f32[56,9,64]{2,0,1:T(8,128)S(1)}, u32[]{:S(2)}, u32[]{:S(2)}) %collective-permute-start.10) | collective-permute-done | bytes 129056 | tf_op jit(solution)/shard_map/ppermute | solution.py:13
  369.8 8.1 %collective-permute-done.11 = f32[56,9,64]{2,0,1:T(8,128)S(1)} collective-permute-done((f32[56,9,64]{2,0,1:T(8,128)S(1)}, f32[56,9,64]{2,0,1:T(8,128)S(1)}, u32[]{:S(2)}, u32[]{:S(2)}) %collective-permute-start.11) | collective-permute-done | bytes 129056 | tf_op jit(solution)/shard_map/ppermute | solution.py:13
  383.2 8.4 %copy.293 = f32[56,9,1152]{0,1,2:T(8,128)} copy(f32[56,9,1152]{2,0,1:T(8,128)} %pad_maximum_fusion.4) | data formatting | bytes 4644864 | tf_op jit(solution)/shard_map/while | solution.py:119
  391.7 51.0 %while.63 = (s32[]{:T(128)}, f32[56,9,640]{2,0,1:T(8,128)S(1)}, s32[]{:T(128)}, s32[]{:T(128)}, f32[56,9,640]{2,0,1:T(8,128)}, /*index=5*/f32[56,9,640]{2,0,1:T(...) while((s32[]{:T(128)}, f32[56,9,640]{2,0,1:T(8,128)S(1)}, ...), condition=%wide.region_43.46_spmd, body=%wide.region_33.45_spmd.sunk | while | flops 178446096 | bytes 18001700 | solution.py:119
  394.5 6.7 gather_fusion.1
  411.5 6.7 gather_fusion.1
  428.5 6.7 gather_fusion.1
  457.8 36.4 %while.64 = (s32[]{:T(128)}, f32[56,9,640]{2,0,1:T(8,128)}, s32[]{:T(128)}, f32[56,9,640]{2,0,1:T(8,128)S(1)}, f32[392,56]{1,0:T(8,128)S(1)}, /*index=5*/f32[3,9...) while((s32[]{:T(128)}, f32[56,9,640]{2,0,1:T(8,128)}, ...), condition=%wide.region_54.57_spmd, body=%wide.region_44.56_spmd.sunk | while | flops 311642496 | bytes 29134816 | solution.py:95
  506.8 61.6 %collective-permute-start.21 = (f32[56,9,64]{2,0,1:T(8,128)S(1)}, f32[56,9,64]{2,0,1:T(8,128)S(1)}, u32[]{:S(2)}, u32[]{:S(2)}) collective-permute-start(f32[56,9,64]{2,0,1:T(8,128)S(1)} %get-tuple-element.746), channel_id=1, source_target_pairs={{0,5},{1,6},{2,7},{3,0},{4,1},{5,2},{6,3},{7,4},{8,13},{9,14},{10,... | collective-permute-start | bytes 387080 | tf_op jit(solution)/shard_map/ppermute | solution.py:13
  570.7 15.8 %collective-permute-done.17 = f32[56,9,64]{2,0,1:T(8,128)S(1)} collective-permute-done((f32[56,9,64]{2,0,1:T(8,128)S(1)}, f32[56,9,64]{2,0,1:T(8,128)S(1)}, u32[]{:S(2)}, u32[]{:S(2)}) %collective-permute-start.17) | collective-permute-done | bytes 129056 | tf_op jit(solution)/shard_map/ppermute | solution.py:13
  589.1 12.8 %collective-permute-done.18 = f32[56,9,64]{2,0,1:T(8,128)S(1)} collective-permute-done((f32[56,9,64]{2,0,1:T(8,128)S(1)}, f32[56,9,64]{2,0,1:T(8,128)S(1)}, u32[]{:S(2)}, u32[]{:S(2)}) %collective-permute-start.18) | collective-permute-done | bytes 129056 | tf_op jit(solution)/shard_map/ppermute | solution.py:13
  602.0 7.1 collective-permute-done.19
  614.4 8.3 %copy.307 = f32[56,9,1152]{0,1,2:T(8,128)} copy(f32[56,9,1152]{2,0,1:T(8,128)} %pad_maximum_fusion.5) | data formatting | bytes 4644864 | tf_op jit(solution)/shard_map/while | solution.py:119
  622.7 47.4 %while.65 = (s32[]{:T(128)}, f32[56,9,640]{2,0,1:T(8,128)}, s32[]{:T(128)}, s32[]{:T(128)}, f32[56,9,640]{2,0,1:T(8,128)S(1)}, /*index=5*/f32[56,9,640]{2,0,1:T(...) while((s32[]{:T(128)}, f32[56,9,640]{2,0,1:T(8,128)}, ...), condition=%wide.region_65.68_spmd, body=%wide.region_55.67_spmd.sunk | while | flops 178446096 | bytes 17336972 | solution.py:119
  624.4 6.7 gather_fusion.2
  640.1 6.7 gather_fusion.2
  655.9 6.7 gather_fusion.2
  681.0 51.6 %all-reduce.3 = (f32[8]{0:T(128)S(1)}, f32[8]{0:T(128)S(1)}, f32[8]{0:T(128)S(1)}) all-reduce(f32[8]{0:T(128)S(1)} %dynamic-update-slice.2, f32[8]{0:T(128)S(1)} %dynamic-update-slice.1, f32[8]{0:T(128)S(1)} %dynamic-update-slice), channel_id=1, replica_groups=mesh['grp'=4,'dom'=8] {'dom'}, use_global_device_ids=true, to_apply=%add.2 | all-reduce | flops 24 | bytes 192
  741.8 57.9 %reduce-scatter.4.cloned.1.call-done = f32[16,27]{1,0:T(8,128)} async-done(((f32[128,27]{1,0:T(8,128)}), f32[16,27]{1,0:T(8,128)}) %reduce-scatter.4.cloned.1.call-update) | async-done | bytes 1744
  (752 shorter events, 336.7 us)
Async XLA Ops:
  7.2 322.5 %copy-start = (f32[56,16]{0,1:T(8,128)S(1)}, f32[56,16]{0,1:T(8,128)}, u32[]{:S(2)}) copy-start(f32[56,16]{0,1:T(8,128)} %param.47) | copy-start | bytes 10756
  7.2 792.5 %reduce-scatter.4.cloned.1.call-start = ((), (), s32[]{:S(2)}) async-start(), calls=%async_computation.1 | async-start | bytes 73728
  25.4 111.8 %collective-permute-start.7 = (f32[56,9,64]{2,0,1:T(8,128)}, f32[56,9,64]{2,0,1:T(8,128)}, u32[]{:S(2)}, u32[]{:S(2)}) collective-permute-start(f32[56,9,64]{2,0,1:T(8,128)} %get-tuple-element.760), channel_id=1, source_target_pairs={{8,0},{16,8},{24,16},{9,1},{17,9},{25,17},{10,2},{18,10},{26,18},{... | collective-permute-start | bytes 387080 | tf_op jit(solution)/shard_map/ppermute | solution.py:19
  26.7 109.5 %collective-permute-start.6 = (f32[56,9,64]{2,0,1:T(8,128)}, f32[56,9,64]{2,0,1:T(8,128)}, u32[]{:S(2)}, u32[]{:S(2)}) collective-permute-start(f32[56,9,64]{2,0,1:T(8,128)} %get-tuple-element.761), channel_id=1, source_target_pairs={{0,8},{8,16},{16,24},{1,9},{9,17},{17,25},{2,10},{10,18},{18,26},{... | collective-permute-start | bytes 387080 | tf_op jit(solution)/shard_map/ppermute | solution.py:19
  30.4 104.8 %collective-permute-start.5 = (f32[56,9,64]{2,0,1:T(8,128)}, f32[56,9,64]{2,0,1:T(8,128)}, u32[]{:S(2)}, u32[]{:S(2)}) collective-permute-start(f32[56,9,64]{2,0,1:T(8,128)} %get-tuple-element.762), channel_id=1, source_target_pairs={{0,5},{1,6},{2,7},{3,0},{4,1},{5,2},{6,3},{7,4},{8,13},{9,14},{10,... | collective-permute-start | bytes 387080 | tf_op jit(solution)/shard_map/ppermute | solution.py:13
  35.4 98.8 %collective-permute-start.4 = (f32[56,9,64]{2,0,1:T(8,128)}, f32[56,9,64]{2,0,1:T(8,128)}, u32[]{:S(2)}, u32[]{:S(2)}) collective-permute-start(f32[56,9,64]{2,0,1:T(8,128)} %get-tuple-element.763), channel_id=1, source_target_pairs={{0,6},{1,7},{2,0},{3,1},{4,2},{5,3},{6,4},{7,5},{8,14},{9,15},{10,... | collective-permute-start | bytes 387080 | tf_op jit(solution)/shard_map/ppermute | solution.py:13
  36.8 45.5 %collective-permute-start = (f32[56,9,64]{2,0,1:T(8,128)}, f32[56,9,64]{2,0,1:T(8,128)}, u32[]{:S(2)}, u32[]{:S(2)}) collective-permute-start(f32[56,9,64]{2,0,1:T(8,128)} %get-tuple-element.767), channel_id=1, source_target_pairs={{0,1},{1,2},{2,3},{3,4},{4,5},{5,6},{6,7},{7,0},{8,9},{9,10},{10,1... | collective-permute-start | bytes 387080 | tf_op jit(solution)/shard_map/ppermute | solution.py:13
  82.2 30.5 %collective-permute-start.1 = (f32[56,9,64]{2,0,1:T(8,128)S(1)}, f32[56,9,64]{2,0,1:T(8,128)S(1)}, u32[]{:S(2)}, u32[]{:S(2)}) collective-permute-start(f32[56,9,64]{2,0,1:T(8,128)S(1)} %copy-done.63), channel_id=1, source_target_pairs={{0,2},{1,3},{2,4},{3,5},{4,6},{5,7},{6,0},{7,1},{8,10},{9,11},{10,... | collective-permute-start | bytes 387080 | tf_op jit(solution)/shard_map/ppermute | solution.py:13
  112.8 14.7 %collective-permute-start.2 = (f32[56,9,64]{2,0,1:T(8,128)S(1)}, f32[56,9,64]{2,0,1:T(8,128)S(1)}, u32[]{:S(2)}, u32[]{:S(2)}) collective-permute-start(f32[56,9,64]{2,0,1:T(8,128)S(1)} %copy-done.62), channel_id=1, source_target_pairs={{0,3},{1,4},{2,5},{3,6},{4,7},{5,0},{6,1},{7,2},{8,11},{9,12},{10,... | collective-permute-start | bytes 387080 | tf_op jit(solution)/shard_map/ppermute | solution.py:13
  127.5 6.7 collective-permute-start.3
  248.4 133.3 %copy-start.6 = (f32[56,9,640]{2,0,1:T(8,128)}, f32[56,9,640]{2,0,1:T(8,128)S(1)}, u32[]{:S(2)}) copy-start(f32[56,9,640]{2,0,1:T(8,128)S(1)} %get-tuple-element.1701) | copy-start | bytes 3870724
  262.9 66.8 %copy-start.74 = (pred[16]{0:T(512)(128)(4,1)S(1)}, pred[16]{0:T(512)(128)(4,1)}, u32[]{:S(2)}) copy-start(pred[16]{0:T(512)(128)(4,1)} %compare_and_fusion.4) | copy-start | bytes 52
  263.0 67.2 %copy-start.79 = (s32[16]{0:T(128)S(1)}, s32[16]{0:T(128)}, u32[]{:S(2)}) copy-start(s32[16]{0:T(128)} %param.46) | copy-start | bytes 196
  263.1 114.9 %collective-permute-start.15 = (f32[56,9,64]{2,0,1:T(8,128)S(1)}, f32[56,9,64]{2,0,1:T(8,128)S(1)}, u32[]{:S(2)}, u32[]{:S(2)}) collective-permute-start(f32[56,9,64]{2,0,1:T(8,128)S(1)} %get-tuple-element.752), channel_id=1, source_target_pairs={{8,0},{16,8},{24,16},{9,1},{17,9},{25,17},{10,2},{18,10},{26,18},{... | collective-permute-start | bytes 387080 | tf_op jit(solution)/shard_map/ppermute | solution.py:19
  264.4 113.6 %collective-permute-start.14 = (f32[56,9,64]{2,0,1:T(8,128)S(1)}, f32[56,9,64]{2,0,1:T(8,128)S(1)}, u32[]{:S(2)}, u32[]{:S(2)}) collective-permute-start(f32[56,9,64]{2,0,1:T(8,128)S(1)} %get-tuple-element.753), channel_id=1, source_target_pairs={{0,8},{8,16},{16,24},{1,9},{9,17},{17,25},{2,10},{10,18},{18,26},{... | collective-permute-start | bytes 387080 | tf_op jit(solution)/shard_map/ppermute | solution.py:19
  267.5 110.5 %collective-permute-start.13 = (f32[56,9,64]{2,0,1:T(8,128)S(1)}, f32[56,9,64]{2,0,1:T(8,128)S(1)}, u32[]{:S(2)}, u32[]{:S(2)}) collective-permute-start(f32[56,9,64]{2,0,1:T(8,128)S(1)} %get-tuple-element.754), channel_id=1, source_target_pairs={{0,5},{1,6},{2,7},{3,0},{4,1},{5,2},{6,3},{7,4},{8,13},{9,14},{10,... | collective-permute-start | bytes 387080 | tf_op jit(solution)/shard_map/ppermute | solution.py:13
  328.0 50.0 %collective-permute-start.12 = (f32[56,9,64]{2,0,1:T(8,128)S(1)}, f32[56,9,64]{2,0,1:T(8,128)S(1)}, u32[]{:S(2)}, u32[]{:S(2)}) collective-permute-start(f32[56,9,64]{2,0,1:T(8,128)S(1)} %get-tuple-element.755), channel_id=1, source_target_pairs={{0,6},{1,7},{2,0},{3,1},{4,2},{5,3},{6,4},{7,5},{8,14},{9,15},{10,... | collective-permute-start | bytes 387080 | tf_op jit(solution)/shard_map/ppermute | solution.py:13
  328.3 18.3 %collective-permute-start.8 = (f32[56,9,64]{2,0,1:T(8,128)S(1)}, f32[56,9,64]{2,0,1:T(8,128)S(1)}, u32[]{:S(2)}, u32[]{:S(2)}) collective-permute-start(f32[56,9,64]{2,0,1:T(8,128)S(1)} %get-tuple-element.759), channel_id=1, source_target_pairs={{0,1},{1,2},{2,3},{3,4},{4,5},{5,6},{6,7},{7,0},{8,9},{9,10},{10,1... | collective-permute-start | bytes 387080 | tf_op jit(solution)/shard_map/ppermute | solution.py:13
  346.6 10.0 %collective-permute-start.9 = (f32[56,9,64]{2,0,1:T(8,128)S(1)}, f32[56,9,64]{2,0,1:T(8,128)S(1)}, u32[]{:S(2)}, u32[]{:S(2)}) collective-permute-start(f32[56,9,64]{2,0,1:T(8,128)S(1)} %get-tuple-element.758), channel_id=1, source_target_pairs={{0,2},{1,3},{2,4},{3,5},{4,6},{5,7},{6,0},{7,1},{8,10},{9,11},{10,... | collective-permute-start | bytes 387080 | tf_op jit(solution)/shard_map/ppermute | solution.py:13
  356.6 13.0 %collective-permute-start.10 = (f32[56,9,64]{2,0,1:T(8,128)S(1)}, f32[56,9,64]{2,0,1:T(8,128)S(1)}, u32[]{:S(2)}, u32[]{:S(2)}) collective-permute-start(f32[56,9,64]{2,0,1:T(8,128)S(1)} %get-tuple-element.757), channel_id=1, source_target_pairs={{0,3},{1,4},{2,5},{3,6},{4,7},{5,0},{6,1},{7,2},{8,11},{9,12},{10,... | collective-permute-start | bytes 387080 | tf_op jit(solution)/shard_map/ppermute | solution.py:13
  369.6 8.3 %collective-permute-start.11 = (f32[56,9,64]{2,0,1:T(8,128)S(1)}, f32[56,9,64]{2,0,1:T(8,128)S(1)}, u32[]{:S(2)}, u32[]{:S(2)}) collective-permute-start(f32[56,9,64]{2,0,1:T(8,128)S(1)} %get-tuple-element.756), channel_id=1, source_target_pairs={{0,7},{1,0},{2,1},{3,2},{4,3},{5,4},{6,5},{7,6},{8,15},{9,8},{10,9... | collective-permute-start | bytes 387080 | tf_op jit(solution)/shard_map/ppermute | solution.py:13
  501.2 67.4 %copy-start.80 = (s32[16]{0:T(128)S(1)}, s32[16]{0:T(128)}, u32[]{:S(2)}) copy-start(s32[16]{0:T(128)} %param.46) | copy-start | bytes 196
  501.2 67.6 %collective-permute-start.16 = (f32[56,9,64]{2,0,1:T(8,128)S(1)}, f32[56,9,64]{2,0,1:T(8,128)S(1)}, u32[]{:S(2)}, u32[]{:S(2)}) collective-permute-start(f32[56,9,64]{2,0,1:T(8,128)S(1)} %get-tuple-element.751), channel_id=1, source_target_pairs={{0,1},{1,2},{2,3},{3,4},{4,5},{5,6},{6,7},{7,0},{8,9},{9,10},{10,1... | collective-permute-start | bytes 387080 | tf_op jit(solution)/shard_map/ppermute | solution.py:13
  502.5 106.7 %collective-permute-start.23 = (f32[56,9,64]{2,0,1:T(8,128)S(1)}, f32[56,9,64]{2,0,1:T(8,128)S(1)}, u32[]{:S(2)}, u32[]{:S(2)}) collective-permute-start(f32[56,9,64]{2,0,1:T(8,128)S(1)} %get-tuple-element.744), channel_id=1, source_target_pairs={{8,0},{16,8},{24,16},{9,1},{17,9},{25,17},{10,2},{18,10},{26,18},{... | collective-permute-start | bytes 387080 | tf_op jit(solution)/shard_map/ppermute | solution.py:19
  503.7 105.4 %collective-permute-start.22 = (f32[56,9,64]{2,0,1:T(8,128)S(1)}, f32[56,9,64]{2,0,1:T(8,128)S(1)}, u32[]{:S(2)}, u32[]{:S(2)}) collective-permute-start(f32[56,9,64]{2,0,1:T(8,128)S(1)} %get-tuple-element.745), channel_id=1, source_target_pairs={{0,8},{8,16},{16,24},{1,9},{9,17},{17,25},{2,10},{10,18},{18,26},{... | collective-permute-start | bytes 387080 | tf_op jit(solution)/shard_map/ppermute | solution.py:19
  506.8 102.3 %collective-permute-start.21 = (f32[56,9,64]{2,0,1:T(8,128)S(1)}, f32[56,9,64]{2,0,1:T(8,128)S(1)}, u32[]{:S(2)}, u32[]{:S(2)}) collective-permute-start(f32[56,9,64]{2,0,1:T(8,128)S(1)} %get-tuple-element.746), channel_id=1, source_target_pairs={{0,5},{1,6},{2,7},{3,0},{4,1},{5,2},{6,3},{7,4},{8,13},{9,14},{10,... | collective-permute-start | bytes 387080 | tf_op jit(solution)/shard_map/ppermute | solution.py:13
  568.4 40.6 %collective-permute-start.20 = (f32[56,9,64]{2,0,1:T(8,128)S(1)}, f32[56,9,64]{2,0,1:T(8,128)S(1)}, u32[]{:S(2)}, u32[]{:S(2)}) collective-permute-start(f32[56,9,64]{2,0,1:T(8,128)S(1)} %get-tuple-element.747), channel_id=1, source_target_pairs={{0,6},{1,7},{2,0},{3,1},{4,2},{5,3},{6,4},{7,5},{8,14},{9,15},{10,... | collective-permute-start | bytes 387080 | tf_op jit(solution)/shard_map/ppermute | solution.py:13
  568.8 17.7 %collective-permute-start.17 = (f32[56,9,64]{2,0,1:T(8,128)S(1)}, f32[56,9,64]{2,0,1:T(8,128)S(1)}, u32[]{:S(2)}, u32[]{:S(2)}) collective-permute-start(f32[56,9,64]{2,0,1:T(8,128)S(1)} %get-tuple-element.750), channel_id=1, source_target_pairs={{0,2},{1,3},{2,4},{3,5},{4,6},{5,7},{6,0},{7,1},{8,10},{9,11},{10,... | collective-permute-start | bytes 387080 | tf_op jit(solution)/shard_map/ppermute | solution.py:13
  586.5 15.3 %collective-permute-start.18 = (f32[56,9,64]{2,0,1:T(8,128)S(1)}, f32[56,9,64]{2,0,1:T(8,128)S(1)}, u32[]{:S(2)}, u32[]{:S(2)}) collective-permute-start(f32[56,9,64]{2,0,1:T(8,128)S(1)} %get-tuple-element.749), channel_id=1, source_target_pairs={{0,3},{1,4},{2,5},{3,6},{4,7},{5,0},{6,1},{7,2},{8,11},{9,12},{10,... | collective-permute-start | bytes 387080 | tf_op jit(solution)/shard_map/ppermute | solution.py:13
  601.9 7.2 collective-permute-start.19
  676.3 63.3 %copy-start.76 = (pred[16]{0:T(512)(128)(4,1)S(1)}, pred[16]{0:T(512)(128)(4,1)}, u32[]{:S(2)}) copy-start(pred[16]{0:T(512)(128)(4,1)} %compare_and_fusion.4) | copy-start | bytes 52
  676.3 63.9 %copy-start.73 = (f32[1,9,128]{2,1,0:T(8,128)S(1)}, f32[1,9,128]{2,1,0:T(8,128)}, u32[]{:S(2)}) copy-start(f32[1,9,128]{2,1,0:T(8,128)} %convolution_bitcast_fusion.8) | copy-start | bytes 13828
  (181 other events, 584.7 us)
Sparse Core Ops, SparseCore 0:
  741.3 58.3 reduce-scatter.3
